TPU v7x, 16 devices: a 4x2x1 block of a 4x4x8 slice. The times are simulated.
16 devices in a mesh: dp: 2 (over y, z), ep: 8 (over x, core).
Axes of the slice: x: 4, y: 2, z: 1, core: 2. Of those that a mesh axis runs over, the one named last changes fastest.
The devices are a block of a 4x4x8 slice.
Arguments:
- tokens: bfloat16 [16, 2048, 2048], P(('dp', 'ep')), parts along dimension 0
- w_gate: bfloat16 [2048, 128], replicated
- expert_ids: int32 [16, 2048, 2], P(('dp', 'ep')), parts along dimension 0
- keep_second: int32 [16, 2048], P(('dp', 'ep')), parts along dimension 0
- w_in: bfloat16 [128, 2048, 768], P('ep')
- w_out: bfloat16 [128, 768, 2048], P('ep')
Outputs:
- output: bfloat16 [16, 2048, 2048], P(('dp', 'ep')), parts along dimension 0
There are 2 independent parts. A program takes and returns all parts, laid end to end along the dimension named above; an argument that names none is the same for every part.
All inputs are finite; a program needn't handle non-finite values.
Results may differ from a plain program's by a relative error of at most 0.001.
Values are sent between devices in bfloat16 or wider.
A program may use at most 768 MiB of HBM per device.

v0:
```python
import jax
import jax.numpy as jnp
from jax import lax
from jax.sharding import PartitionSpec as P


def build_routing(tokens, w_gate, expert_ids, keep_second, capacity):
    expert_count = w_gate.shape[1]
    logits = jnp.einsum("gsm,me->gse", tokens, w_gate, preferred_element_type=jnp.float32)
    gate_probs = jax.nn.softmax(logits, axis=-1)
    first_hot = jax.nn.one_hot(expert_ids[:, :, 0], expert_count, dtype=jnp.int32)
    second_hot = jax.nn.one_hot(expert_ids[:, :, 1], expert_count, dtype=jnp.int32) * keep_second[:, :, None]
    gate_first = jnp.sum(gate_probs * first_hot, axis=-1)
    gate_second = jnp.sum(gate_probs * second_hot, axis=-1)
    gate_total = gate_first + gate_second
    pos_first = jnp.sum((jnp.cumsum(first_hot, axis=1) - first_hot) * first_hot, axis=-1)
    second_base = jnp.cumsum(second_hot, axis=1) - second_hot + jnp.sum(first_hot, axis=1, keepdims=True)
    pos_second = jnp.sum(second_base * second_hot, axis=-1)
    slot_first = first_hot.astype(jnp.bfloat16)[:, :, :, None] * jax.nn.one_hot(pos_first, capacity, dtype=jnp.bfloat16)[:, :, None, :]
    slot_second = second_hot.astype(jnp.bfloat16)[:, :, :, None] * jax.nn.one_hot(pos_second, capacity, dtype=jnp.bfloat16)[:, :, None, :]
    dispatch = slot_first + slot_second
    weight_first = (gate_first / gate_total).astype(jnp.bfloat16)[:, :, None, None]
    weight_second = (gate_second / gate_total).astype(jnp.bfloat16)[:, :, None, None]
    combine = weight_first * slot_first + weight_second * slot_second
    return dispatch, combine


def solution(mesh):
    group_count = mesh.shape["ep"]

    def local_layer(tokens, w_gate, expert_ids, keep_second, w_in, w_out):
        token_count = tokens.shape[1]
        model_dim = tokens.shape[2]
        expert_count = w_gate.shape[1]
        local_experts = w_in.shape[0]
        capacity = 2 * token_count // expert_count
        dispatch, combine = build_routing(tokens, w_gate, expert_ids, keep_second, capacity)
        send_rows = jnp.einsum("gsec,gsm->ecm", dispatch, tokens, preferred_element_type=jnp.float32).astype(jnp.bfloat16)
        send_rows = send_rows.reshape(group_count, local_experts, capacity, model_dim)
        recv_rows = lax.all_to_all(send_rows, "ep", 0, 0, tiled=True)
        hidden = jax.nn.relu(jnp.einsum("gecm,emh->egch", recv_rows, w_in, preferred_element_type=jnp.float32)).astype(jnp.bfloat16)
        back_rows = jnp.einsum("egch,ehm->gecm", hidden, w_out, preferred_element_type=jnp.float32).astype(jnp.bfloat16)
        back_rows = lax.all_to_all(back_rows, "ep", 0, 0, tiled=True)
        back_rows = back_rows.reshape(expert_count, capacity, model_dim)
        mixed_rows = jnp.einsum("gsec,ecm->gsm", combine, back_rows, preferred_element_type=jnp.float32)
        return mixed_rows.astype(jnp.bfloat16)

    group_spec = P(("dp", "ep"))
    return jax.shard_map(local_layer, mesh=mesh, in_specs=(group_spec, P(), group_spec, group_spec, P("ep"), P("ep")), out_specs=group_spec, check_vma=False)
```

profile of v0, /device:TPU:113, one launch (start us, length us, event | category | flops | bytes accessed | tf_op | source)
XLA Modules:
  0.0 613.4 jit_solution(7304807917694033773)
XLA Ops:
  0.0 0.0 copy-start
  0.0 0.8 fusion.63
  0.8 0.3 fusion.53
  1.2 0.6 fusion.51
  1.8 0.3 copy.21
  2.1 1.3 fusion.54
  3.5 0.6 fusion.49
  4.1 0.3 copy.24
  4.4 1.6 select_convert_fusion
  6.0 0.9 convert_convert_fusion
  7.0 1.3 copy.22
  8.3 2.0 copy.19
  10.4 0.1 broadcast.219
  10.4 1.2 fusion.48
  11.7 0.1 broadcast.221
  11.7 0.0 copy-done.2
  11.8 1.0 fusion.46
  12.8 44.3 %fusion.10 = bf16[128,32,2048]{2,0,1:T(8,128)(2,1)} fusion(bf16[1,2048,2048]{2,1,0:T(8,128)(2,1)} %param.6, bf16[2048,32]{0,1:T(8,128)(2,1)S(1)} %get-tuple-element.16, bf16[2048,128]{1,0:T(8,128)(2,1)S(1)} %copy.22, bf16[2048,32]{0,1:T(8,128)(2,1)S(1)} %get-tuple-element.15, bf16[2048,128]{1,0:T(8,128)(2,1)} %copy.19), kind=kOutput, calls=%fused_computation.14 | convolution fusion | flops 34393292800 | bytes 26476544 | tf_op jit(solution)/shard_map/gsec,gsm->ecm/dot_general | solution.py:38
  57.2 8.0 %copy.26 = bf16[8,16,32,2048]{3,1,2,0:T(8,128)(2,1)S(1)} copy(bf16[8,16,32,2048]{3,1,0,2:T(8,128)(2,1)} %bitcast.80) | data formatting | bytes 33554432 | tf_op jit(solution)/shard_map/reshape | solution.py:39
  65.2 189.3 %all_to_all.10 = bf16[8,16,32,2048]{3,1,2,0:T(8,128)(2,1)} all-to-all(bf16[8,16,32,2048]{3,1,2,0:T(8,128)(2,1)S(1)} %copy.26), channel_id=1, replica_groups=mesh['dp'=2,'ep'=8] {'ep'}, dimensions={0} | all-to-all | bytes 33554432 | tf_op jit(solution)/shard_map/all_to_all | solution.py:40
  254.5 59.7 %maximum_convert_fusion.4 = bf16[16,8,32,768]{3,2,1,0:T(8,128)(2,1)} fusion(bf16[16,2048,768]{2,1,0:T(8,128)(2,1)} %param.10, bf16[8,16,32,2048]{3,1,2,0:T(8,128)(2,1)} %all_to_all.10), kind=kOutput, calls=%fused_computation.15.clone.clone.1 | convolution fusion | flops 12891193344 | bytes 73400320 | tf_op jit(solution)/shard_map/gecm,emh->egch/dot_general | solution.py:41
  314.2 26.7 %convert_bitcast_fusion = bf16[8,16,32,2048]{3,2,0,1:T(8,128)(2,1)} fusion(bf16[16,768,2048]{2,1,0:T(8,128)(2,1)} %param.11, bf16[16,8,32,768]{3,2,1,0:T(8,128)(2,1)} %maximum_convert_fusion.4), kind=kOutput, calls=%fused_computation.13 | convolution fusion | flops 12893290496 | bytes 73400320 | tf_op jit(solution)/shard_map/egch,ehm->gecm/dot_general | solution.py:42
  340.9 14.1 %copy.28 = bf16[8,16,32,2048]{3,2,1,0:T(8,128)(2,1)} copy(bf16[8,16,32,2048]{3,2,0,1:T(8,128)(2,1)} %convert_bitcast_fusion) | data formatting | bytes 33554432 | tf_op jit(solution)/shard_map/convert_element_type | solution.py:42
  355.0 6.7 %all-to-all-start.1 = ((bf16[8,16,32,2048]{3,2,1,0:T(8,128)(2,1)}), bf16[8,16,32,2048]{3,2,1,0:T(8,128)(2,1)}, u32[]{:S(2)}, u32[]{:S(2)}) async-start(bf16[8,16,32,2048]{3,2,1,0:T(8,128)(2,1)} %copy.28), calls=%async_computation.1 | async-start | bytes 33554432 | tf_op jit(solution)/shard_map/all_to_all | solution.py:43
  361.7 0.0 copy-done
  361.7 6.3 %fusion.64 = (f32[2048]{0:T(1024)S(1)}, f32[2048,128]{0,1:T(8,128)S(1)}) fusion(bf16[2048,128]{1,0:T(8,128)(2,1)S(1)} %copy-done, bf16[1,2048,2048]{2,1,0:T(8,128)(2,1)} %param.6), kind=kOutput, calls=%fused_computation.74 | convolution fusion | flops 1074001920 | bytes 9969664 | tf_op jit(solution)/shard_map/gsm,me->gse/dot_general | solution.py:9
  368.0 0.2 fusion.56
  368.2 0.5 fusion.43
  368.7 0.0 copy-done.1
  368.7 22.3 %fusion.78 = bf16[2048,128,32]{1,0,2:T(8,128)(2,1)} fusion(bf16[2048,32]{0,1:T(8,128)(2,1)S(1)} %get-tuple-element.16, bf16[2048,128]{1,0:T(8,128)(2,1)S(1)} %copy.22, bf16[2048]{0:T(1024)(128)(2,1)S(1)} %get-tuple-element.10, bf16[2048,32]{0,1:T(8,128)(2,1)S(1)} %get-tuple-element.15, bf16[2048,128]{1,0:T(8,128)(2,1)S(1)} %copy-done.1, ...), kind=kLoop, calls=%fused_computation.7.clone.clone.clone.clone.1 | loop fusion | flops 41943040 | bytes 18096128 | tf_op jit(solution)/shard_map/gsec,ecm->gsm/dot_general | solution.py:45
  391.0 154.2 %all-to-all-done.1 = bf16[8,16,32,2048]{3,2,1,0:T(8,128)(2,1)} async-done(((bf16[8,16,32,2048]{3,2,1,0:T(8,128)(2,1)}), bf16[8,16,32,2048]{3,2,1,0:T(8,128)(2,1)}, u32[]{:S(2)}, u32[]{:S(2)}) %all-to-all-start.1) | async-done | bytes 16777248 | tf_op jit(solution)/shard_map/all_to_all | solution.py:43
  545.2 67.8 %fusion.13 = bf16[1,2048,2048]{2,1,0:T(8,128)(2,1)} fusion(bf16[128,32,2048]{2,1,0:T(8,128)(2,1)} %bitcast.25, bf16[2048,128,32]{1,0,2:T(8,128)(2,1)} %fusion.78), kind=kOutput, calls=%fused_computation.16 | convolution fusion | flops 34363932672 | bytes 41943040 | tf_op jit(solution)/shard_map/gsec,ecm->gsm/dot_general | solution.py:45
  (10 shorter events, 0.1 us)
Async XLA Ops:
  0.0 361.7 %copy-start = (bf16[2048,128]{1,0:T(8,128)(2,1)S(1)}, bf16[2048,128]{1,0:T(8,128)(2,1)}, u32[]{:S(2)}) copy-start(bf16[2048,128]{1,0:T(8,128)(2,1)} %param.7) | copy-start | bytes 1572868
  0.0 11.7 %copy-start.2 = (s32[1,2048]{1,0:T(1,128)S(1)}, s32[1,2048]{1,0:T(1,128)}, u32[]{:S(2)}) copy-start(s32[1,2048]{1,0:T(1,128)} %param.9) | copy-start | bytes 24580
  355.0 190.2 %all-to-all-start.1 = ((bf16[8,16,32,2048]{3,2,1,0:T(8,128)(2,1)}), bf16[8,16,32,2048]{3,2,1,0:T(8,128)(2,1)}, u32[]{:S(2)}, u32[]{:S(2)}) async-start(bf16[8,16,32,2048]{3,2,1,0:T(8,128)(2,1)} %copy.28), calls=%async_computation.1 | async-start | bytes 33554432 | tf_op jit(solution)/shard_map/all_to_all | solution.py:43
  361.7 7.0 %copy-start.1 = (bf16[2048,128]{1,0:T(8,128)(2,1)S(1)}, bf16[2048,128]{1,0:T(8,128)(2,1)}, u32[]{:S(2)}) copy-start(bf16[2048,128]{1,0:T(8,128)(2,1)} %copy.19) | copy-start | bytes 1572868
where the time goes:
time: 618 us; the launch traced here: 613 us
  matrix products  205 us (33%)
  blocking collectives  189 us (31%)
  waiting for transfers between devices  154 us (25%)
  other arithmetic  30.6 us (5%)
  local copies, waits for them, and re-layouts  27.2 us (4%)
  starting transfers between devices  6.68 us (1%)
    all_to_all x1, blocking collectives, local_layer(): recv_rows = lax.all_to_all(send_rows, 'ep', 0, 0, tiled=True)  189 us
    all_to_all x1, waiting for transfers between devices, local_layer(): back_rows = lax.all_to_all(back_rows, 'ep', 0, 0, tiled=True)  154 us
    dot_general x1, matrix products, local_layer(): jnp.einsum('gsec,ecm->gsm', combine, back_rows, preferred_element_type=jn...  67.8 us
    dot_general x1, matrix products, local_layer(): jnp.einsum('gecm,emh->egch', recv_rows, w_in, preferred_element_type=jnp....  59.7 us
    dot_general x1, matrix products, local_layer(): jnp.einsum('gsec,gsm->ecm', dispatch, tokens, preferred_element_type=jnp....  44.3 us
    dot_general x1, matrix products, local_layer(): jnp.einsum('egch,ehm->gecm', hidden, w_out, preferred_element_type=jnp.fl...  26.7 us
    dot_general x1, other arithmetic, local_layer(): jnp.einsum('gsec,ecm->gsm', combine, back_rows, preferred_element_type=jn...  22.3 us
    convert_element_type x1, local copies, waits for them, and re-layouts, local_layer(): jnp.einsum('egch,ehm->gecm', hidden, w_out, preferred_element_type=jnp.fl...  14.1 us
  transfers between devices with their start and end apart: 1, of which 1 were waited for; matrix products, arithmetic and copies ran while one was open for 5% of the time, Pallas kernels for 0%

commit v1 on v0

v1 whole, which is shorter than its diff:
```python
import functools

import jax
import jax.numpy as jnp
from jax import lax
from jax.experimental import pallas as pl
from jax.experimental.pallas import tpu as pltpu
from jax.sharding import PartitionSpec as P

MESH = pl.DeviceIdType.MESH
LAG = 3
TILE = 256


def ring_offsets(chip_count):
    near = sorted(range(1, chip_count), key=lambda d: min(d, chip_count - d))
    return near


def moe_kernel(
    n, sizes, ids_ref, keep_ref, x_hbm, wg_ref, win_hbm, wout_hbm, out_hbm,
    x_v, acc, win_v, wout_v, fsend, frecv, ysend, yrecv, dmat, hid, crow, colb,
    x_sem, win_sem, wout_sem, fs_sem, fr_sem, ys_sem, yr_sem, out_sem,
):
    tokens, model, hidden, experts, local, capacity = sizes
    rows = n * capacity
    fslots, yslots = frecv.shape[0], yrecv.shape[0]
    shift = (local - 1).bit_length()
    blocks = tokens // TILE
    me = lax.axis_index("ep")

    x_copy = pltpu.make_async_copy(x_hbm.at[0], x_v, x_sem)

    def weight_copies(k):
        b = lax.rem(k, 2)
        return (
            pltpu.make_async_copy(win_hbm.at[k], win_v.at[b], win_sem.at[b]),
            pltpu.make_async_copy(wout_hbm.at[k], wout_v.at[b], wout_sem.at[b]),
        )

    def owner_rows(d):
        return pl.ds(pl.multiple_of(d * capacity, capacity), capacity)

    cores = 2 if n % 2 == 0 else 1
    chips = n // cores
    my_chip, my_core = me // cores, lax.rem(me, cores)
    targets = []
    for dist in ring_offsets(chips) + [0]:
        for c in range(cores):
            if dist == 0 and c == 0:
                continue
            targets.append(lax.rem(my_chip + dist, chips) * cores + lax.rem(my_core + c, cores))

    def send(src, src_slot, dst, dst_slot, s_sem, r_sem):
        for d in targets:
            pltpu.make_async_remote_copy(
                src_ref=src.at[src_slot, owner_rows(d)],
                dst_ref=dst.at[dst_slot, owner_rows(me)],
                send_sem=s_sem.at[src_slot],
                recv_sem=r_sem.at[dst_slot],
                device_id={"ep": d},
                device_id_type=MESH,
            ).start()

    def all_peers(src, src_slot, dst, dst_slot, s_sem, r_sem):
        part = pl.ds(0, (n - 1) * capacity)
        return pltpu.make_async_remote_copy(
            src_ref=src.at[src_slot, part],
            dst_ref=dst.at[dst_slot, part],
            send_sem=s_sem.at[src_slot],
            recv_sem=r_sem.at[dst_slot],
            device_id={"ep": me},
            device_id_type=MESH,
        )

    def fwd_args(k):
        return (fsend, lax.rem(k, 2), frecv, lax.rem(k, fslots), fs_sem, fr_sem)

    def back_args(k):
        return (ysend, lax.rem(k, 2), yrecv, lax.rem(k, yslots), ys_sem, yr_sem)

    def keep_own(src, src_slot, dst, dst_slot, *_):
        dst[dst_slot, owner_rows(me), :] = src[src_slot, owner_rows(me), :]

    def hot(blk, expert_row):
        return lax.broadcasted_iota(jnp.int32, (experts, TILE), 0) == expert_row

    def load_ids(b):
        cols = pl.ds(b * TILE, TILE)
        return ids_ref[0:1, cols], ids_ref[1:2, cols], keep_ref[0:1, cols] == 1

    def route():
        count = jnp.zeros((experts, TILE), jnp.float32)
        for b in range(blocks):
            i1, _, _ = load_ids(b)
            count = count + hot(b, i1).astype(jnp.float32)
        base1 = jnp.zeros((experts, 1), jnp.float32)
        base2 = jnp.sum(count, axis=1, keepdims=True)
        before = (
            lax.broadcasted_iota(jnp.int32, (TILE, TILE), 0) < lax.broadcasted_iota(jnp.int32, (TILE, TILE), 1)
        ).astype(jnp.bfloat16)
        for b in range(blocks):
            i1, i2, k2 = load_ids(b)
            hot1 = hot(b, i1).astype(jnp.float32)
            hot2 = jnp.where(k2, hot(b, i2).astype(jnp.float32), 0.0)
            ahead1 = jnp.dot(hot1.astype(jnp.bfloat16), before, preferred_element_type=jnp.float32) + base1
            ahead2 = jnp.dot(hot2.astype(jnp.bfloat16), before, preferred_element_type=jnp.float32) + base2
            base1 = base1 + jnp.sum(hot1, axis=1, keepdims=True)
            base2 = base2 + jnp.sum(hot2, axis=1, keepdims=True)
            pos1 = jnp.sum(ahead1 * hot1, axis=0, keepdims=True)
            pos2 = jnp.sum(ahead2 * hot2, axis=0, keepdims=True)

            def code(e, pos, kept):
                home = (e & (local - 1)) * rows + (e >> shift) * capacity
                return jnp.where(kept, home.astype(jnp.float32) + pos, -1.0)

            cols = pl.ds(b * TILE, TILE)
            crow[0:1, cols] = code(i1, pos1, pos1 < capacity)
            crow[1:2, cols] = code(i2, pos2, jnp.logical_and(k2, pos2 < capacity))

    def gates():
        for b in range(blocks):
            cols = pl.ds(b * TILE, TILE)
            i1, i2, k2 = load_ids(b)
            logits = jnp.dot(x_v[cols, :], wg_ref[...], preferred_element_type=jnp.float32).T
            top = jnp.max(logits, axis=0, keepdims=True)
            grown = jnp.exp(logits - top)
            probs = grown / jnp.sum(grown, axis=0, keepdims=True)
            g1 = jnp.sum(jnp.where(hot(b, i1), probs, 0.0), axis=0, keepdims=True)
            g2 = jnp.where(k2, jnp.sum(jnp.where(hot(b, i2), probs, 0.0), axis=0, keepdims=True), 0.0)
            total = g1 + g2
            for q, row in enumerate((crow[0:1, cols], crow[1:2, cols], g1 / total, g2 / total)):
                colb[q, cols, :] = jnp.broadcast_to(row, (128, TILE)).T

    def dispatch(k):
        slot = lax.rem(k, 2)
        base = (k * rows).astype(jnp.float32)
        for b in range(blocks):
            cols = pl.ds(b * TILE, TILE)
            want = lax.broadcasted_iota(jnp.int32, (rows, TILE), 0).astype(jnp.float32)
            c1, c2 = crow[0:1, cols] - base, crow[1:2, cols] - base
            dmat[:, cols] = jnp.where(jnp.logical_or(c1 == want, c2 == want), 1.0, 0.0).astype(jnp.bfloat16)

        @pl.loop(0, model // TILE)
        def _(j):
            cols = pl.ds(pl.multiple_of(j * TILE, TILE), TILE)
            fsend[slot, :, cols] = jnp.dot(
                dmat[...], x_v[:, cols], preferred_element_type=jnp.float32
            ).astype(jnp.bfloat16)

    def experts_ffn(k):
        w, slot, out_slot = lax.rem(k, 2), lax.rem(k, fslots), lax.rem(k, 2)

        @pl.loop(0, hidden // TILE)
        def _(j):
            cols = pl.ds(pl.multiple_of(j * TILE, TILE), TILE)
            h = jnp.dot(frecv[slot], win_v[w, :, cols], preferred_element_type=jnp.float32)
            hid[:, cols] = jnp.maximum(h, 0.0).astype(jnp.bfloat16)

        @pl.loop(0, model // TILE)
        def _(j):
            cols = pl.ds(pl.multiple_of(j * TILE, TILE), TILE)
            y = jnp.dot(hid[...], wout_v[w, :, cols], preferred_element_type=jnp.float32)
            ysend[out_slot, :, cols] = y.astype(jnp.bfloat16)

    def mix_weights(k, toks):
        base = (k * rows).astype(jnp.float32)
        c1, c2 = colb[0, toks, :] - base, colb[1, toks, :] - base
        w1, w2 = colb[2, toks, :], colb[3, toks, :]
        parts = []
        for lane in range(0, rows, 128):
            want = (lax.broadcasted_iota(jnp.int32, (TILE, 128), 1) + lane).astype(jnp.float32)
            parts.append((jnp.where(c1 == want, w1, 0.0) + jnp.where(c2 == want, w2, 0.0)).astype(jnp.bfloat16))
        return jnp.concatenate(parts, axis=1)

    def combine(k, last):
        slot = lax.rem(k, yslots)

        @pl.loop(0, blocks)
        def _(i):
            toks = pl.ds(pl.multiple_of(i * TILE, TILE), TILE)
            mix = mix_weights(k, toks)
            for j in range(0, model, 2 * TILE):
                cols = pl.ds(j, 2 * TILE)
                got = acc[toks, cols] + jnp.dot(mix, yrecv[slot, :, cols], preferred_element_type=jnp.float32)
                if last:
                    x_v[toks, cols] = got.astype(jnp.bfloat16)
                else:
                    acc[toks, cols] = got
            if last:
                pltpu.make_async_copy(x_v.at[toks], out_hbm.at[0, toks], out_sem).start()

    x_copy.start()
    for copy in weight_copies(0):
        copy.start()
    barrier = pltpu.get_barrier_semaphore()
    for d in targets:
        pl.semaphore_signal(barrier, inc=1, device_id={"ep": d}, device_id_type=MESH)
    route()
    x_copy.wait()
    dispatch(jnp.int32(0))
    pl.semaphore_wait(barrier, n - 1)

    @pl.loop(0, local + LAG)
    def _(t):
        @pl.when(t >= LAG)
        def _():
            all_peers(*back_args(t - LAG)).wait_recv()

        @pl.when(t < local)
        def _():
            send(*fwd_args(t))
            keep_own(*fwd_args(t))

        @pl.when(t == 1)
        def _():
            gates()

            @pl.loop(0, blocks)
            def _(i):
                acc[pl.ds(pl.multiple_of(i * TILE, TILE), TILE), :] = jnp.zeros((TILE, model), jnp.float32)

        @pl.when(jnp.logical_and(t >= LAG, t < local + LAG - 1))
        def _():
            combine(t - LAG, False)

        @pl.when(jnp.logical_and(t >= 1, t <= local))
        def _():
            k = t - 1

            @pl.when(t < local)
            def _():
                for copy in weight_copies(t):
                    copy.start()

            for copy in weight_copies(k):
                copy.wait()
            all_peers(*fwd_args(k)).wait_recv()

            @pl.when(k >= 2)
            def _():
                all_peers(*back_args(k - 2)).wait_send()

            experts_ffn(k)
            send(*back_args(k))
            keep_own(*back_args(k))

        @pl.when(t + 1 < local)
        def _():
            @pl.when(t >= 1)
            def _():
                all_peers(*fwd_args(t - 1)).wait_send()

            dispatch(t + 1)

    combine(jnp.int32(local - 1), True)
    for k in range(max(local - 2, 0), local):
        all_peers(*fwd_args(jnp.int32(k))).wait_send()
        all_peers(*back_args(jnp.int32(k))).wait_send()
    pltpu.make_async_copy(x_v, out_hbm.at[0], out_sem).wait()


def solution(mesh):
    n = mesh.shape["ep"]

    def local_layer(tokens, w_gate, expert_ids, keep_second, w_in, w_out):
        _, token_count, model = tokens.shape
        experts = w_gate.shape[1]
        local, _, hidden = w_in.shape
        capacity = 2 * token_count // experts
        rows = n * capacity
        bf16, f32 = jnp.bfloat16, jnp.float32
        sizes = (token_count, model, hidden, experts, local, capacity)
        vmem, hbm = pl.BlockSpec(memory_space=pltpu.VMEM), pl.BlockSpec(memory_space=pl.ANY)
        dma = pltpu.SemaphoreType.DMA
        return pl.pallas_call(
            functools.partial(moe_kernel, n, sizes),
            out_shape=jax.ShapeDtypeStruct(tokens.shape, bf16),
            in_specs=[vmem, vmem, hbm, vmem, hbm, hbm],
            out_specs=hbm,
            scratch_shapes=[
                pltpu.VMEM((token_count, model), bf16),
                pltpu.VMEM((token_count, model), f32),
                pltpu.VMEM((2, model, hidden), bf16),
                pltpu.VMEM((2, hidden, model), bf16),
                pltpu.VMEM((2, rows, model), bf16),
                pltpu.VMEM((LAG, rows, model), bf16),
                pltpu.VMEM((2, rows, model), bf16),
                pltpu.VMEM((LAG + 1, rows, model), bf16),
                pltpu.VMEM((rows, token_count), bf16),
                pltpu.VMEM((rows, hidden), bf16),
                pltpu.VMEM((8, token_count), f32),
                pltpu.VMEM((4, token_count, 128), f32),
                dma,
                dma((2,)),
                dma((2,)),
                dma((2,)),
                dma((LAG,)),
                dma((2,)),
                dma((LAG + 1,)),
                dma,
            ],
            compiler_params=pltpu.CompilerParams(
                collective_id=0, has_side_effects=True, vmem_limit_bytes=63 * 1024 * 1024
            ),
        )(expert_ids[0].T, keep_second, tokens, w_gate, w_in, w_out)

    group_spec = P(("dp", "ep"))
    return jax.shard_map(
        local_layer,
        mesh=mesh,
        in_specs=(group_spec, P(), group_spec, group_spec, P("ep"), P("ep")),
        out_specs=group_spec,
        check_vma=False,
    )
```

time: 618 us -> 387 us (0.63)
  Pallas kernels: 0 us -> 378 us
  matrix products: 205 us -> 0 us
  blocking collectives: 189 us -> 0 us
  waiting for transfers between devices: 154 us -> 0 us
  other arithmetic: 30.6 us -> 0 us
  local copies, waits for them, and re-layouts: 27.2 us -> 8.44 us
  starting transfers between devices: 6.68 us -> 0 us
    pallas_call x0 -> x1, Pallas kernels: none -> 378 us  [local_layer(): pl.pallas_call(functools.partial(moe_kernel, n, sizes), out_shape=jax.Sha...]
    dot_general x5 -> x0, matrix products: 205 us -> none  [the longest x1 67.8 us: local_layer(): jnp.einsum('gsec,ecm->gsm', combine, back_rows, preferred_element_type=jn...]
    all_to_all x1 -> x0, blocking collectives: 189 us -> none  [local_layer(): recv_rows = lax.all_to_all(send_rows, 'ep', 0, 0, tiled=True)]
    all_to_all x1 -> x0, waiting for transfers between devices: 154 us -> none  [local_layer(): back_rows = lax.all_to_all(back_rows, 'ep', 0, 0, tiled=True)]
    dot_general x1 -> x0, other arithmetic: 22.3 us -> none  [local_layer(): jnp.einsum('gsec,ecm->gsm', combine, back_rows, preferred_element_type=jn...]
    convert_element_type x3 -> x0, local copies, waits for them, and re-layouts: 17.5 us -> none  [the longest x1 14.1 us: local_layer(): jnp.einsum('egch,ehm->gecm', hidden, w_out, preferred_element_type=jnp.fl...]
    unnamed x6 -> x1, local copies, waits for them, and re-layouts: 0.01 us -> 8.44 us
    reshape x1 -> x0, local copies, waits for them, and re-layouts: 8.03 us -> none  [local_layer(): send_rows.reshape(group_count, local_experts, capacity, model_dim)]
  transfers between devices with their start and end apart: 1 -> 0, of which waited for: 1 -> 0; matrix products, arithmetic and copies ran while one was open for 5% -> 0% of each run, Pallas kernels for 0% -> 0%
where the time goes in v1:
time: 387 us
  Pallas kernels  378 us (98%)
  local copies, waits for them, and re-layouts  8.44 us (2%)
    pallas_call x1, Pallas kernels, local_layer(): pl.pallas_call(functools.partial(moe_kernel, n, sizes), out_shape=jax.Sha...  378 us
    unnamed x1, local copies, waits for them, and re-layouts  8.44 us

profile of v1, /device:TPU:113, one launch (start us, length us, event | category | flops | bytes accessed | tf_op | source)
XLA Modules:
  0.0 386.6 jit_solution(12864296388216965654)
XLA Ops:
  0.0 378.2 %shard_map.64 = bf16[1,2048,2048]{2,1,0:T(8,128)(2,1)} custom-call(s32[2,2048]{1,0:T(2,128)} %bitcast.3, s32[1,2048]{1,0:T(1,128)} %keep_ref.1, bf16[1,2048,2048]{2,1,0:T(8,128)(2,1)} %x_hbm.1, bf16[2048,128]{1,0:T(8,128)(2,1)} %wg_ref.1, bf16[16,2048,768]{2,1,0:T(8,128)(2,1)} %win_hbm.1, bf16[16,768,2048]{2,1,0:T(8,128)(2,1)} %wout_hbm.1), custom_call_target="tpu_custom_call" | custom-call | tf_op jit(solution)/shard_map/pallas_call | solution.py:276
  378.2 8.4 %copy.8 = bf16[1,2048,2048]{2,1,0:T(8,128)(2,1)} copy(bf16[1,2048,2048]{2,1,0:T(8,128)(2,1)} %shard_map.64) | data formatting | bytes 16777216

commit v2 on v1

--- a/solution.py
+++ b/solution.py
@@ -10,6 +10,8 @@
 MESH = pl.DeviceIdType.MESH
 LAG = 3
 TILE = 256
+VMEM_A = 36 * 1024 * 1024
+VMEM_B = 12 * 1024 * 1024
 
 
 def ring_offsets(chip_count):
@@ -17,10 +19,44 @@
     return near
 
 
+def mix_weights(colb, base, rows, toks):
+    base = jnp.int32(base).astype(jnp.float32)
+    c1, c2 = colb[0, toks, :] - base, colb[1, toks, :] - base
+    w1, w2 = colb[2, toks, :], colb[3, toks, :]
+    parts = []
+    for lane in range(0, rows, 128):
+        want = (lax.broadcasted_iota(jnp.int32, (TILE, 128), 1) + lane).astype(jnp.float32)
+        parts.append((jnp.where(c1 == want, w1, 0.0) + jnp.where(c2 == want, w2, 0.0)).astype(jnp.bfloat16))
+    return jnp.concatenate(parts, axis=1)
+
+
+def last_kernel(base, acc, colb, yrecv, out_hbm, stage, sem):
+    tokens, model = acc.shape
+    yslots, rows, _ = yrecv.shape
+    slot = (base // rows) % yslots
+
+    def out_copy(i):
+        toks = pl.ds(pl.multiple_of(i * TILE, TILE), TILE)
+        return pltpu.make_async_copy(stage.at[toks], out_hbm.at[0, toks], sem)
+
+    @pl.loop(0, tokens // TILE)
+    def _(i):
+        toks = pl.ds(pl.multiple_of(i * TILE, TILE), TILE)
+        mix = mix_weights(colb, base, rows, toks)
+        for j in range(0, model, 2 * TILE):
+            cols = pl.ds(j, 2 * TILE)
+            got = acc[toks, cols] + jnp.dot(mix, yrecv[slot, :, cols], preferred_element_type=jnp.float32)
+            stage[toks, cols] = got.astype(jnp.bfloat16)
+        out_copy(i).start()
+
+    pltpu.make_async_copy(stage, out_hbm.at[0], sem).wait()
+
+
 def moe_kernel(
-    n, sizes, ids_ref, keep_ref, x_hbm, wg_ref, win_hbm, wout_hbm, out_hbm,
-    x_v, acc, win_v, wout_v, fsend, frecv, ysend, yrecv, dmat, hid, crow, colb,
-    x_sem, win_sem, wout_sem, fs_sem, fr_sem, ys_sem, yr_sem, out_sem,
+    n, sizes, ids_ref, keep_ref, x_hbm, wg_hbm, win_hbm, wout_hbm,
+    acc, colb, yrecv,
+    x_v, wg_v, win_v, wout_v, fsend, frecv, ysend, dmat, hid, crow,
+    x_sem, wg_sem, win_sem, wout_sem, fs_sem, fr_sem, ys_sem, yr_sem,
 ):
     tokens, model, hidden, experts, local, capacity = sizes
     rows = n * capacity
@@ -29,7 +65,11 @@
     blocks = tokens // TILE
     me = lax.axis_index("ep")
 
-    x_copy = pltpu.make_async_copy(x_hbm.at[0], x_v, x_sem)
+    def x_copy(j):
+        cols = pl.ds(pl.multiple_of(j * TILE, TILE), TILE)
+        return pltpu.make_async_copy(x_hbm.at[0, :, cols], x_v.at[:, cols], x_sem.at[j])
+
+    wg_copy = pltpu.make_async_copy(wg_hbm, wg_v, wg_sem)
 
     def weight_copies(k):
         b = lax.rem(k, 2)
@@ -122,7 +162,7 @@
         for b in range(blocks):
             cols = pl.ds(b * TILE, TILE)
             i1, i2, k2 = load_ids(b)
-            logits = jnp.dot(x_v[cols, :], wg_ref[...], preferred_element_type=jnp.float32).T
+            logits = jnp.dot(x_v[cols, :], wg_v[...], preferred_element_type=jnp.float32).T
             top = jnp.max(logits, axis=0, keepdims=True)
             grown = jnp.exp(logits - top)
             probs = grown / jnp.sum(grown, axis=0, keepdims=True)
@@ -132,7 +172,7 @@
             for q, row in enumerate((crow[0:1, cols], crow[1:2, cols], g1 / total, g2 / total)):
                 colb[q, cols, :] = jnp.broadcast_to(row, (128, TILE)).T
 
-    def dispatch(k):
+    def dispatch(k, first=False):
         slot = lax.rem(k, 2)
         base = (k * rows).astype(jnp.float32)
         for b in range(blocks):
@@ -143,6 +183,8 @@
 
         @pl.loop(0, model // TILE)
         def _(j):
+            if first:
+                x_copy(j).wait()
             cols = pl.ds(pl.multiple_of(j * TILE, TILE), TILE)
             fsend[slot, :, cols] = jnp.dot(
                 dmat[...], x_v[:, cols], preferred_element_type=jnp.float32
@@ -163,42 +205,27 @@
             y = jnp.dot(hid[...], wout_v[w, :, cols], preferred_element_type=jnp.float32)
             ysend[out_slot, :, cols] = y.astype(jnp.bfloat16)
 
-    def mix_weights(k, toks):
-        base = (k * rows).astype(jnp.float32)
-        c1, c2 = colb[0, toks, :] - base, colb[1, toks, :] - base
-        w1, w2 = colb[2, toks, :], colb[3, toks, :]
-        parts = []
-        for lane in range(0, rows, 128):
-            want = (lax.broadcasted_iota(jnp.int32, (TILE, 128), 1) + lane).astype(jnp.float32)
-            parts.append((jnp.where(c1 == want, w1, 0.0) + jnp.where(c2 == want, w2, 0.0)).astype(jnp.bfloat16))
-        return jnp.concatenate(parts, axis=1)
-
-    def combine(k, last):
-        slot = lax.rem(k, yslots)
-
+    def combine(k):
         @pl.loop(0, blocks)
         def _(i):
             toks = pl.ds(pl.multiple_of(i * TILE, TILE), TILE)
-            mix = mix_weights(k, toks)
+            mix = mix_weights(colb, k * rows, rows, toks)
             for j in range(0, model, 2 * TILE):
                 cols = pl.ds(j, 2 * TILE)
-                got = acc[toks, cols] + jnp.dot(mix, yrecv[slot, :, cols], preferred_element_type=jnp.float32)
-                if last:
-                    x_v[toks, cols] = got.astype(jnp.bfloat16)
-                else:
-                    acc[toks, cols] = got
-            if last:
-                pltpu.make_async_copy(x_v.at[toks], out_hbm.at[0, toks], out_sem).start()
-
-    x_copy.start()
-    for copy in weight_copies(0):
-        copy.start()
+                acc[toks, cols] += jnp.dot(
+                    mix, yrecv[lax.rem(k, yslots), :, cols], preferred_element_type=jnp.float32
+                )
+
+    for j in range(model // TILE):
+        x_copy(j).start()
     barrier = pltpu.get_barrier_semaphore()
     for d in targets:
         pl.semaphore_signal(barrier, inc=1, device_id={"ep": d}, device_id_type=MESH)
     route()
-    x_copy.wait()
-    dispatch(jnp.int32(0))
+    wg_copy.start()
+    for copy in weight_copies(0):
+        copy.start()
+    dispatch(jnp.int32(0), first=True)
     pl.semaphore_wait(barrier, n - 1)
 
     @pl.loop(0, local + LAG)
@@ -214,6 +241,7 @@
 
         @pl.when(t == 1)
         def _():
+            wg_copy.wait()
             gates()
 
             @pl.loop(0, blocks)
@@ -222,7 +250,7 @@
 
         @pl.when(jnp.logical_and(t >= LAG, t < local + LAG - 1))
         def _():
-            combine(t - LAG, False)
+            combine(t - LAG)
 
         @pl.when(jnp.logical_and(t >= 1, t <= local))
         def _():
@@ -253,11 +281,9 @@
 
             dispatch(t + 1)
 
-    combine(jnp.int32(local - 1), True)
     for k in range(max(local - 2, 0), local):
         all_peers(*fwd_args(jnp.int32(k))).wait_send()
         all_peers(*back_args(jnp.int32(k))).wait_send()
-    pltpu.make_async_copy(x_v, out_hbm.at[0], out_sem).wait()
 
 
 def solution(mesh):
@@ -273,24 +299,27 @@
         sizes = (token_count, model, hidden, experts, local, capacity)
         vmem, hbm = pl.BlockSpec(memory_space=pltpu.VMEM), pl.BlockSpec(memory_space=pl.ANY)
         dma = pltpu.SemaphoreType.DMA
-        return pl.pallas_call(
+        acc, colb, yrecv = pl.pallas_call(
             functools.partial(moe_kernel, n, sizes),
-            out_shape=jax.ShapeDtypeStruct(tokens.shape, bf16),
-            in_specs=[vmem, vmem, hbm, vmem, hbm, hbm],
-            out_specs=hbm,
+            out_shape=(
+                pltpu.VMEM((token_count, model), f32),
+                pltpu.VMEM((4, token_count, 128), f32),
+                pltpu.VMEM((LAG + 1, rows, model), bf16),
+            ),
+            in_specs=[vmem, vmem, hbm, hbm, hbm, hbm],
+            out_specs=(vmem, vmem, vmem),
             scratch_shapes=[
                 pltpu.VMEM((token_count, model), bf16),
-                pltpu.VMEM((token_count, model), f32),
+                pltpu.VMEM(w_gate.shape, bf16),
                 pltpu.VMEM((2, model, hidden), bf16),
                 pltpu.VMEM((2, hidden, model), bf16),
                 pltpu.VMEM((2, rows, model), bf16),
                 pltpu.VMEM((LAG, rows, model), bf16),
                 pltpu.VMEM((2, rows, model), bf16),
-                pltpu.VMEM((LAG + 1, rows, model), bf16),
                 pltpu.VMEM((rows, token_count), bf16),
                 pltpu.VMEM((rows, hidden), bf16),
                 pltpu.VMEM((8, token_count), f32),
-                pltpu.VMEM((4, token_count, 128), f32),
+                dma((model // TILE,)),
                 dma,
                 dma((2,)),
                 dma((2,)),
@@ -298,12 +327,19 @@
                 dma((LAG,)),
                 dma((2,)),
                 dma((LAG + 1,)),
-                dma,
             ],
             compiler_params=pltpu.CompilerParams(
-                collective_id=0, has_side_effects=True, vmem_limit_bytes=63 * 1024 * 1024
+                collective_id=0, has_side_effects=True, vmem_limit_bytes=VMEM_A
             ),
         )(expert_ids[0].T, keep_second, tokens, w_gate, w_in, w_out)
+        return pl.pallas_call(
+            functools.partial(last_kernel, (local - 1) * rows),
+            out_shape=jax.ShapeDtypeStruct(tokens.shape, bf16),
+            in_specs=[vmem, vmem, vmem],
+            out_specs=hbm,
+            scratch_shapes=[pltpu.VMEM((token_count, model), bf16), dma],
+            compiler_params=pltpu.CompilerParams(vmem_limit_bytes=VMEM_B),
+        )(acc, colb, yrecv)
 
     group_spec = P(("dp", "ep"))
     return jax.shard_map(

time: 387 us -> 376 us (0.972)
  local copies, waits for them, and re-layouts: 8.44 us -> 0 us
    unnamed x1 -> x0, local copies, waits for them, and re-layouts: 8.44 us -> none
    pallas_call x1 -> x2, Pallas kernels: 378 us -> 376 us  [the longest x1 371 us: local_layer(): pl.pallas_call(functools.partial(moe_kernel, n, sizes), out_shape=(pltpu....]
where the time goes in v2:
time: 376 us
  Pallas kernels  376 us (100%)
    pallas_call x1, Pallas kernels, local_layer(): pl.pallas_call(functools.partial(moe_kernel, n, sizes), out_shape=(pltpu....  371 us

profile of v2, /device:TPU:113, one launch (start us, length us, event | category | flops | bytes accessed | tf_op | source)
XLA Modules:
  0.0 375.8 jit_solution(13286692826671977363)
XLA Ops:
  0.0 371.2 %shard_map.64 = (f32[2048,2048]{1,0:T(8,128)S(1)}, f32[4,2048,128]{2,1,0:T(8,128)S(1)}, bf16[4,256,2048]{2,1,0:T(8,128)(2,1)S(1)}) custom-call(s32[2,2048]{1,0:T(2,128)} %bitcast.3, s32[1,2048]{1,0:T(1,128)} %keep_ref.1, bf16[1,2048,2048]{2,1,0:T(8,128)(2,1)} %x_hbm.1, bf16[2048,128]{1,0:T(8,128)(2,1)} %wg_hbm.1, bf16[16,2048,768]{2,1,0:T(8,128)(2,1)} %win_hbm.1, ...), custom_call_target="tpu_custom_call" | custom-call | tf_op jit(solution)/shard_map/pallas_call | solution.py:302
  371.2 4.5 %shard_map.65 = bf16[1,2048,2048]{2,1,0:T(8,128)(2,1)} custom-call(f32[2048,2048]{1,0:T(8,128)S(1)} %get-tuple-element.8.acc, f32[4,2048,128]{2,1,0:T(8,128)S(1)} %get-tuple-element.9.colb, bf16[4,256,2048]{2,1,0:T(8,128)(2,1)S(1)} %get-tuple-element.10.yrecv), custom_call_target="tpu_custom_call" | custom-call | tf_op jit(solution)/shard_map/pallas_call | solution.py:335

commit v3 on v2

--- a/solution.py
+++ b/solution.py
@@ -10,6 +10,7 @@
 MESH = pl.DeviceIdType.MESH
 LAG = 3
 TILE = 256
+PIECE = 512
 VMEM_A = 36 * 1024 * 1024
 VMEM_B = 12 * 1024 * 1024
 
@@ -53,10 +54,10 @@
 
 
 def moe_kernel(
-    n, sizes, ids_ref, keep_ref, x_hbm, wg_hbm, win_hbm, wout_hbm,
+    n, sizes, ids_hbm, keep_hbm, x_hbm, wg_hbm, win_hbm, wout_hbm,
     acc, colb, yrecv,
-    x_v, wg_v, win_v, wout_v, fsend, frecv, ysend, dmat, hid, crow,
-    x_sem, wg_sem, win_sem, wout_sem, fs_sem, fr_sem, ys_sem, yr_sem,
+    ids_ref, keep_ref, x_v, wg_v, win_v, wout_v, fsend, frecv, ysend, dmat, hid, crow,
+    id_sem, x_sem, wg_sem, win_sem, wout_sem, fs_sem, fr_sem, ys_sem, yr_sem,
 ):
     tokens, model, hidden, experts, local, capacity = sizes
     rows = n * capacity
@@ -69,6 +70,10 @@
         cols = pl.ds(pl.multiple_of(j * TILE, TILE), TILE)
         return pltpu.make_async_copy(x_hbm.at[0, :, cols], x_v.at[:, cols], x_sem.at[j])
 
+    id_copies = (
+        pltpu.make_async_copy(ids_hbm, ids_ref, id_sem.at[0]),
+        pltpu.make_async_copy(keep_hbm, keep_ref, id_sem.at[1]),
+    )
     wg_copy = pltpu.make_async_copy(wg_hbm, wg_v, wg_sem)
 
     def weight_copies(k):
@@ -91,11 +96,11 @@
                 continue
             targets.append(lax.rem(my_chip + dist, chips) * cores + lax.rem(my_core + c, cores))
 
-    def send(src, src_slot, dst, dst_slot, s_sem, r_sem):
+    def send(src, src_slot, dst, dst_slot, s_sem, r_sem, cols=slice(None)):
         for d in targets:
             pltpu.make_async_remote_copy(
-                src_ref=src.at[src_slot, owner_rows(d)],
-                dst_ref=dst.at[dst_slot, owner_rows(me)],
+                src_ref=src.at[src_slot, owner_rows(d), cols],
+                dst_ref=dst.at[dst_slot, owner_rows(me), cols],
                 send_sem=s_sem.at[src_slot],
                 recv_sem=r_sem.at[dst_slot],
                 device_id={"ep": d},
@@ -172,8 +177,7 @@
             for q, row in enumerate((crow[0:1, cols], crow[1:2, cols], g1 / total, g2 / total)):
                 colb[q, cols, :] = jnp.broadcast_to(row, (128, TILE)).T
 
-    def dispatch(k, first=False):
-        slot = lax.rem(k, 2)
+    def dispatch_mask(k):
         base = (k * rows).astype(jnp.float32)
         for b in range(blocks):
             cols = pl.ds(b * TILE, TILE)
@@ -181,14 +185,16 @@
             c1, c2 = crow[0:1, cols] - base, crow[1:2, cols] - base
             dmat[:, cols] = jnp.where(jnp.logical_or(c1 == want, c2 == want), 1.0, 0.0).astype(jnp.bfloat16)
 
+    def dispatch_tile(slot, j):
+        cols = pl.ds(pl.multiple_of(j * TILE, TILE), TILE)
+        fsend[slot, :, cols] = jnp.dot(dmat[...], x_v[:, cols], preferred_element_type=jnp.float32).astype(jnp.bfloat16)
+
+    def dispatch(k):
+        dispatch_mask(k)
+
         @pl.loop(0, model // TILE)
         def _(j):
-            if first:
-                x_copy(j).wait()
-            cols = pl.ds(pl.multiple_of(j * TILE, TILE), TILE)
-            fsend[slot, :, cols] = jnp.dot(
-                dmat[...], x_v[:, cols], preferred_element_type=jnp.float32
-            ).astype(jnp.bfloat16)
+            dispatch_tile(lax.rem(k, 2), j)
 
     def experts_ffn(k):
         w, slot, out_slot = lax.rem(k, 2), lax.rem(k, fslots), lax.rem(k, 2)
@@ -216,17 +222,31 @@
                     mix, yrecv[lax.rem(k, yslots), :, cols], preferred_element_type=jnp.float32
                 )
 
+    for copy in id_copies:
+        copy.start()
     for j in range(model // TILE):
         x_copy(j).start()
     barrier = pltpu.get_barrier_semaphore()
     for d in targets:
         pl.semaphore_signal(barrier, inc=1, device_id={"ep": d}, device_id_type=MESH)
+    for copy in id_copies:
+        copy.wait()
     route()
     wg_copy.start()
     for copy in weight_copies(0):
         copy.start()
-    dispatch(jnp.int32(0), first=True)
+    first = jnp.int32(0)
+    dispatch_mask(first)
     pl.semaphore_wait(barrier, n - 1)
+
+    @pl.loop(0, model // PIECE)
+    def _(piece):
+        for j in range(PIECE // TILE):
+            x_copy(piece * (PIECE // TILE) + j).wait()
+            dispatch_tile(0, piece * (PIECE // TILE) + j)
+        send(*fwd_args(first), pl.ds(pl.multiple_of(piece * PIECE, PIECE), PIECE))
+
+    keep_own(*fwd_args(first))
 
     @pl.loop(0, local + LAG)
     def _(t):
@@ -234,7 +254,7 @@
         def _():
             all_peers(*back_args(t - LAG)).wait_recv()
 
-        @pl.when(t < local)
+        @pl.when(jnp.logical_and(t >= 1, t < local))
         def _():
             send(*fwd_args(t))
             keep_own(*fwd_args(t))
@@ -306,9 +326,11 @@
                 pltpu.VMEM((4, token_count, 128), f32),
                 pltpu.VMEM((LAG + 1, rows, model), bf16),
             ),
-            in_specs=[vmem, vmem, hbm, hbm, hbm, hbm],
+            in_specs=[hbm] * 6,
             out_specs=(vmem, vmem, vmem),
             scratch_shapes=[
+                pltpu.VMEM((2, token_count), jnp.int32),
+                pltpu.VMEM((1, token_count), jnp.int32),
                 pltpu.VMEM((token_count, model), bf16),
                 pltpu.VMEM(w_gate.shape, bf16),
                 pltpu.VMEM((2, model, hidden), bf16),
@@ -319,6 +341,7 @@
                 pltpu.VMEM((rows, token_count), bf16),
                 pltpu.VMEM((rows, hidden), bf16),
                 pltpu.VMEM((8, token_count), f32),
+                dma((2,)),
                 dma((model // TILE,)),
                 dma,
                 dma((2,)),

time: 376 us -> 376 us (level)
  no operation moved by 1% of the time
where the time goes in v3:
time: 376 us
  Pallas kernels  376 us (100%)
    pallas_call x1, Pallas kernels, local_layer(): pl.pallas_call(functools.partial(moe_kernel, n, sizes), out_shape=(pltpu....  371 us

profile of v3, /device:TPU:113, one launch (start us, length us, event | category | flops | bytes accessed | tf_op | source)
XLA Modules:
  0.0 375.7 jit_solution(13279381101184154443)
XLA Ops:
  0.0 371.1 %shard_map.64 = (f32[2048,2048]{1,0:T(8,128)S(1)}, f32[4,2048,128]{2,1,0:T(8,128)S(1)}, bf16[4,256,2048]{2,1,0:T(8,128)(2,1)S(1)}) custom-call(s32[2,2048]{1,0:T(2,128)} %bitcast.3, s32[1,2048]{1,0:T(1,128)} %keep_hbm.1, bf16[1,2048,2048]{2,1,0:T(8,128)(2,1)} %x_hbm.1, bf16[2048,128]{1,0:T(8,128)(2,1)} %wg_hbm.1, bf16[16,2048,768]{2,1,0:T(8,128)(2,1)} %win_hbm.1, ...), custom_call_target="tpu_custom_call" | custom-call | tf_op jit(solution)/shard_map/pallas_call | solution.py:322
  371.1 4.5 %shard_map.65 = bf16[1,2048,2048]{2,1,0:T(8,128)(2,1)} custom-call(f32[2048,2048]{1,0:T(8,128)S(1)} %get-tuple-element.8.acc, f32[4,2048,128]{2,1,0:T(8,128)S(1)} %get-tuple-element.9.colb, bf16[4,256,2048]{2,1,0:T(8,128)(2,1)S(1)} %get-tuple-element.10.yrecv), custom_call_target="tpu_custom_call" | custom-call | tf_op jit(solution)/shard_map/pallas_call | solution.py:358

commit v4 on v3

--- a/solution.py
+++ b/solution.py
@@ -8,7 +8,9 @@
 from jax.sharding import PartitionSpec as P
 
 MESH = pl.DeviceIdType.MESH
-LAG = 3
+FFN_LAG = 2
+LAG = 4
+RESULTS = 3
 TILE = 256
 PIECE = 512
 VMEM_A = 36 * 1024 * 1024
@@ -122,7 +124,7 @@
         return (fsend, lax.rem(k, 2), frecv, lax.rem(k, fslots), fs_sem, fr_sem)
 
     def back_args(k):
-        return (ysend, lax.rem(k, 2), yrecv, lax.rem(k, yslots), ys_sem, yr_sem)
+        return (ysend, lax.rem(k, RESULTS), yrecv, lax.rem(k, yslots), ys_sem, yr_sem)
 
     def keep_own(src, src_slot, dst, dst_slot, *_):
         dst[dst_slot, owner_rows(me), :] = src[src_slot, owner_rows(me), :]
@@ -197,7 +199,7 @@
             dispatch_tile(lax.rem(k, 2), j)
 
     def experts_ffn(k):
-        w, slot, out_slot = lax.rem(k, 2), lax.rem(k, fslots), lax.rem(k, 2)
+        w, slot, out_slot = lax.rem(k, 2), lax.rem(k, fslots), lax.rem(k, RESULTS)
 
         @pl.loop(0, hidden // TILE)
         def _(j):
@@ -272,22 +274,22 @@
         def _():
             combine(t - LAG)
 
-        @pl.when(jnp.logical_and(t >= 1, t <= local))
-        def _():
-            k = t - 1
-
-            @pl.when(t < local)
+        @pl.when(jnp.logical_and(t >= FFN_LAG, t < local + FFN_LAG))
+        def _():
+            k = t - FFN_LAG
+
+            @pl.when(k + 1 < local)
             def _():
-                for copy in weight_copies(t):
+                for copy in weight_copies(k + 1):
                     copy.start()
 
             for copy in weight_copies(k):
                 copy.wait()
             all_peers(*fwd_args(k)).wait_recv()
 
-            @pl.when(k >= 2)
+            @pl.when(k >= RESULTS)
             def _():
-                all_peers(*back_args(k - 2)).wait_send()
+                all_peers(*back_args(k - RESULTS)).wait_send()
 
             experts_ffn(k)
             send(*back_args(k))
@@ -303,6 +305,7 @@
 
     for k in range(max(local - 2, 0), local):
         all_peers(*fwd_args(jnp.int32(k))).wait_send()
+    for k in range(max(local - RESULTS, 0), local):
         all_peers(*back_args(jnp.int32(k))).wait_send()
 
 
@@ -337,7 +340,7 @@
                 pltpu.VMEM((2, hidden, model), bf16),
                 pltpu.VMEM((2, rows, model), bf16),
                 pltpu.VMEM((LAG, rows, model), bf16),
-                pltpu.VMEM((2, rows, model), bf16),
+                pltpu.VMEM((RESULTS, rows, model), bf16),
                 pltpu.VMEM((rows, token_count), bf16),
                 pltpu.VMEM((rows, hidden), bf16),
                 pltpu.VMEM((8, token_count), f32),
@@ -348,7 +351,7 @@
                 dma((2,)),
                 dma((2,)),
                 dma((LAG,)),
-                dma((2,)),
+                dma((RESULTS,)),
                 dma((LAG + 1,)),
             ],
             compiler_params=pltpu.CompilerParams(

time: 376 us -> 387 us (1.029)
  local copies, waits for them, and re-layouts: 0 us -> 11.5 us
    unnamed x0 -> x4, local copies, waits for them, and re-layouts: none -> 11.5 us
where the time goes in v4:
time: 387 us
  Pallas kernels  376 us (97%)
  local copies, waits for them, and re-layouts  11.5 us (3%)
    pallas_call x1, Pallas kernels, local_layer(): pl.pallas_call(functools.partial(moe_kernel, n, sizes), out_shape=(pltpu....  371 us
    unnamed x4, local copies, waits for them, and re-layouts  11.5 us

profile of v4, /device:TPU:113, one launch (start us, length us, event | category | flops | bytes accessed | tf_op | source)
XLA Modules:
  0.0 387.2 jit_solution(11992916017657722655)
XLA Ops:
  0.0 371.1 %shard_map.64 = (f32[2048,2048]{1,0:T(8,128)S(1)}, f32[4,2048,128]{2,1,0:T(8,128)S(1)}, bf16[5,256,2048]{2,1,0:T(8,128)(2,1)S(1)}) custom-call(s32[2,2048]{1,0:T(2,128)} %bitcast.3, s32[1,2048]{1,0:T(1,128)} %keep_hbm.1, bf16[1,2048,2048]{2,1,0:T(8,128)(2,1)} %x_hbm.1, bf16[2048,128]{1,0:T(8,128)(2,1)} %wg_hbm.1, bf16[16,2048,768]{2,1,0:T(8,128)(2,1)} %win_hbm.1, ...), custom_call_target="tpu_custom_call" | custom-call | tf_op jit(solution)/shard_map/pallas_call | solution.py:325
  371.1 0.0 copy-start
  371.2 5.7 %copy-done = f32[2048,2048]{1,0:T(8,128)} copy-done((f32[2048,2048]{1,0:T(8,128)}, f32[2048,2048]{1,0:T(8,128)S(1)}, u32[]{:S(2)}) %copy-start) | copy-done | bytes 16777240
  376.9 0.0 copy-start.1
  376.9 5.8 %copy-done.1 = f32[2048,2048]{1,0:T(8,128)S(1)} copy-done((f32[2048,2048]{1,0:T(8,128)S(1)}, f32[2048,2048]{1,0:T(8,128)}, u32[]{:S(2)}) %copy-start.1) | copy-done | bytes 16777240
  382.6 4.5 %shard_map.65 = bf16[1,2048,2048]{2,1,0:T(8,128)(2,1)} custom-call(f32[2048,2048]{1,0:T(8,128)S(1)} %copy-done.1, f32[4,2048,128]{2,1,0:T(8,128)S(1)} %get-tuple-element.9.colb, bf16[5,256,2048]{2,1,0:T(8,128)(2,1)S(1)} %get-tuple-element.10.yrecv), custom_call_target="tpu_custom_call" | custom-call | tf_op jit(solution)/shard_map/pallas_call | solution.py:361
Async XLA Ops:
  371.1 5.7 %copy-start = (f32[2048,2048]{1,0:T(8,128)}, f32[2048,2048]{1,0:T(8,128)S(1)}, u32[]{:S(2)}) copy-start(f32[2048,2048]{1,0:T(8,128)S(1)} %get-tuple-element.8.acc) | copy-start | bytes 50331652
  376.9 5.8 %copy-start.1 = (f32[2048,2048]{1,0:T(8,128)S(1)}, f32[2048,2048]{1,0:T(8,128)}, u32[]{:S(2)}) copy-start(f32[2048,2048]{1,0:T(8,128)} %copy-done) | copy-start | bytes 50331652

commit v5 on v3

--- a/solution.py
+++ b/solution.py
@@ -10,7 +10,7 @@
 MESH = pl.DeviceIdType.MESH
 LAG = 3
 TILE = 256
-PIECE = 512
+PIECE = 256
 VMEM_A = 36 * 1024 * 1024
 VMEM_B = 12 * 1024 * 1024
 
@@ -31,10 +31,8 @@
     return jnp.concatenate(parts, axis=1)
 
 
-def last_kernel(base, acc, colb, yrecv, out_hbm, stage, sem):
+def last_kernel(slot, acc, mix_last, yrecv, out_hbm, stage, sem):
     tokens, model = acc.shape
-    yslots, rows, _ = yrecv.shape
-    slot = (base // rows) % yslots
 
     def out_copy(i):
         toks = pl.ds(pl.multiple_of(i * TILE, TILE), TILE)
@@ -43,10 +41,9 @@
     @pl.loop(0, tokens // TILE)
     def _(i):
         toks = pl.ds(pl.multiple_of(i * TILE, TILE), TILE)
-        mix = mix_weights(colb, base, rows, toks)
         for j in range(0, model, 2 * TILE):
             cols = pl.ds(j, 2 * TILE)
-            got = acc[toks, cols] + jnp.dot(mix, yrecv[slot, :, cols], preferred_element_type=jnp.float32)
+            got = acc[toks, cols] + jnp.dot(mix_last[toks, :], yrecv[slot, :, cols], preferred_element_type=jnp.float32)
             stage[toks, cols] = got.astype(jnp.bfloat16)
         out_copy(i).start()
 
@@ -55,8 +52,8 @@
 
 def moe_kernel(
     n, sizes, ids_hbm, keep_hbm, x_hbm, wg_hbm, win_hbm, wout_hbm,
-    acc, colb, yrecv,
-    ids_ref, keep_ref, x_v, wg_v, win_v, wout_v, fsend, frecv, ysend, dmat, hid, crow,
+    acc, mix_last, yrecv,
+    ids_ref, keep_ref, x_v, wg_v, win_v, wout_v, fsend, frecv, ysend, dmat, hid, crow, colb,
     id_sem, x_sem, wg_sem, win_sem, wout_sem, fs_sem, fr_sem, ys_sem, yr_sem,
 ):
     tokens, model, hidden, experts, local, capacity = sizes
@@ -134,7 +131,7 @@
         cols = pl.ds(b * TILE, TILE)
         return ids_ref[0:1, cols], ids_ref[1:2, cols], keep_ref[0:1, cols] == 1
 
-    def route():
+    def route(on_block):
         count = jnp.zeros((experts, TILE), jnp.float32)
         for b in range(blocks):
             i1, _, _ = load_ids(b)
@@ -145,6 +142,7 @@
             lax.broadcasted_iota(jnp.int32, (TILE, TILE), 0) < lax.broadcasted_iota(jnp.int32, (TILE, TILE), 1)
         ).astype(jnp.bfloat16)
         for b in range(blocks):
+            on_block(b)
             i1, i2, k2 = load_ids(b)
             hot1 = hot(b, i1).astype(jnp.float32)
             hot2 = jnp.where(k2, hot(b, i2).astype(jnp.float32), 0.0)
@@ -224,17 +222,20 @@
 
     for copy in id_copies:
         copy.start()
-    for j in range(model // TILE):
-        x_copy(j).start()
+    x_copy(0).start()
     barrier = pltpu.get_barrier_semaphore()
     for d in targets:
         pl.semaphore_signal(barrier, inc=1, device_id={"ep": d}, device_id_type=MESH)
     for copy in id_copies:
         copy.wait()
-    route()
-    wg_copy.start()
-    for copy in weight_copies(0):
-        copy.start()
+    tiles = model // TILE
+    ahead = min(4, tiles - 1)
+
+    def next_tile(b):
+        if b % 2 == 0 and 1 + b // 2 <= ahead:
+            x_copy(1 + b // 2).start()
+
+    route(next_tile)
     first = jnp.int32(0)
     dispatch_mask(first)
     pl.semaphore_wait(barrier, n - 1)
@@ -242,11 +243,20 @@
     @pl.loop(0, model // PIECE)
     def _(piece):
         for j in range(PIECE // TILE):
-            x_copy(piece * (PIECE // TILE) + j).wait()
-            dispatch_tile(0, piece * (PIECE // TILE) + j)
+            tile = piece * (PIECE // TILE) + j
+            x_copy(tile).wait()
+
+            @pl.when(tile + ahead + 1 < tiles)
+            def _():
+                x_copy(tile + ahead + 1).start()
+
+            dispatch_tile(0, tile)
         send(*fwd_args(first), pl.ds(pl.multiple_of(piece * PIECE, PIECE), PIECE))
 
     keep_own(*fwd_args(first))
+    wg_copy.start()
+    for copy in weight_copies(first):
+        copy.start()
 
     @pl.loop(0, local + LAG)
     def _(t):
@@ -271,6 +281,13 @@
         @pl.when(jnp.logical_and(t >= LAG, t < local + LAG - 1))
         def _():
             combine(t - LAG)
+
+        @pl.when(t == local)
+        def _():
+            @pl.loop(0, blocks)
+            def _(i):
+                toks = pl.ds(pl.multiple_of(i * TILE, TILE), TILE)
+                mix_last[toks, :] = mix_weights(colb, (local - 1) * rows, rows, toks)
 
         @pl.when(jnp.logical_and(t >= 1, t <= local))
         def _():
@@ -319,11 +336,11 @@
         sizes = (token_count, model, hidden, experts, local, capacity)
         vmem, hbm = pl.BlockSpec(memory_space=pltpu.VMEM), pl.BlockSpec(memory_space=pl.ANY)
         dma = pltpu.SemaphoreType.DMA
-        acc, colb, yrecv = pl.pallas_call(
+        acc, mix_last, yrecv = pl.pallas_call(
             functools.partial(moe_kernel, n, sizes),
             out_shape=(
                 pltpu.VMEM((token_count, model), f32),
-                pltpu.VMEM((4, token_count, 128), f32),
+                pltpu.VMEM((token_count, rows), bf16),
                 pltpu.VMEM((LAG + 1, rows, model), bf16),
             ),
             in_specs=[hbm] * 6,
@@ -341,6 +358,7 @@
                 pltpu.VMEM((rows, token_count), bf16),
                 pltpu.VMEM((rows, hidden), bf16),
                 pltpu.VMEM((8, token_count), f32),
+                pltpu.VMEM((4, token_count, 128), f32),
                 dma((2,)),
                 dma((model // TILE,)),
                 dma,
@@ -356,13 +374,13 @@
             ),
         )(expert_ids[0].T, keep_second, tokens, w_gate, w_in, w_out)
         return pl.pallas_call(
-            functools.partial(last_kernel, (local - 1) * rows),
+            functools.partial(last_kernel, (local - 1) % (LAG + 1)),
             out_shape=jax.ShapeDtypeStruct(tokens.shape, bf16),
             in_specs=[vmem, vmem, vmem],
             out_specs=hbm,
             scratch_shapes=[pltpu.VMEM((token_count, model), bf16), dma],
             compiler_params=pltpu.CompilerParams(vmem_limit_bytes=VMEM_B),
-        )(acc, colb, yrecv)
+        )(acc, mix_last, yrecv)
 
     group_spec = P(("dp", "ep"))
     return jax.shard_map(

time: 376 us -> 373 us (level)
  Pallas kernels: 376 us -> 372 us
where the time goes in v5:
time: 373 us; the launch traced here: 372 us
  Pallas kernels  372 us (100%)
    pallas_call x1, Pallas kernels, local_layer(): pl.pallas_call(functools.partial(moe_kernel, n, sizes), out_shape=(pltpu....  368 us

profile of v5, /device:TPU:113, one launch (start us, length us, event | category | flops | bytes accessed | tf_op | source)
XLA Modules:
  0.0 372.4 jit_solution(9578000947806307541)
XLA Ops:
  0.0 367.9 %shard_map.64 = (f32[2048,2048]{1,0:T(8,128)S(1)}, bf16[2048,256]{1,0:T(8,128)(2,1)S(1)}, bf16[4,256,2048]{2,1,0:T(8,128)(2,1)S(1)}) custom-call(s32[2,2048]{1,0:T(2,128)} %bitcast.3, s32[1,2048]{1,0:T(1,128)} %keep_hbm.1, bf16[1,2048,2048]{2,1,0:T(8,128)(2,1)} %x_hbm.1, bf16[2048,128]{1,0:T(8,128)(2,1)} %wg_hbm.1, bf16[16,2048,768]{2,1,0:T(8,128)(2,1)} %win_hbm.1, ...), custom_call_target="tpu_custom_call" | custom-call | tf_op jit(solution)/shard_map/pallas_call | solution.py:339
  367.9 4.5 %shard_map.65 = bf16[1,2048,2048]{2,1,0:T(8,128)(2,1)} custom-call(f32[2048,2048]{1,0:T(8,128)S(1)} %get-tuple-element.8.acc, bf16[2048,256]{1,0:T(8,128)(2,1)S(1)} %get-tuple-element.9.mix_last, bf16[4,256,2048]{2,1,0:T(8,128)(2,1)S(1)} %get-tuple-element.10.yrecv), custom_call_target="tpu_custom_call" | custom-call | tf_op jit(solution)/shard_map/pallas_call | solution.py:376

commit v6 on v5

--- a/solution.py
+++ b/solution.py
@@ -16,8 +16,7 @@
 
 
 def ring_offsets(chip_count):
-    near = sorted(range(1, chip_count), key=lambda d: min(d, chip_count - d))
-    return near
+    return sorted(range(1, chip_count), key=lambda d: -min(d, chip_count - d))
 
 
 def mix_weights(colb, base, rows, toks):

time: 373 us -> 372 us (level)
  no operation moved by 1% of the time
where the time goes in v6:
time: 372 us
  Pallas kernels  372 us (100%)
    pallas_call x1, Pallas kernels, local_layer(): pl.pallas_call(functools.partial(moe_kernel, n, sizes), out_shape=(pltpu....  367 us

profile of v6, /device:TPU:113, one launch (start us, length us, event | category | flops | bytes accessed | tf_op | source)
XLA Modules:
  0.0 371.6 jit_solution(17517057831585591911)
XLA Ops:
  0.0 367.1 %shard_map.64 = (f32[2048,2048]{1,0:T(8,128)S(1)}, bf16[2048,256]{1,0:T(8,128)(2,1)S(1)}, bf16[4,256,2048]{2,1,0:T(8,128)(2,1)S(1)}) custom-call(s32[2,2048]{1,0:T(2,128)} %bitcast.3, s32[1,2048]{1,0:T(1,128)} %keep_hbm.1, bf16[1,2048,2048]{2,1,0:T(8,128)(2,1)} %x_hbm.1, bf16[2048,128]{1,0:T(8,128)(2,1)} %wg_hbm.1, bf16[16,2048,768]{2,1,0:T(8,128)(2,1)} %win_hbm.1, ...), custom_call_target="tpu_custom_call" | custom-call | tf_op jit(solution)/shard_map/pallas_call | solution.py:338
  367.1 4.5 %shard_map.65 = bf16[1,2048,2048]{2,1,0:T(8,128)(2,1)} custom-call(f32[2048,2048]{1,0:T(8,128)S(1)} %get-tuple-element.8.acc, bf16[2048,256]{1,0:T(8,128)(2,1)S(1)} %get-tuple-element.9.mix_last, bf16[4,256,2048]{2,1,0:T(8,128)(2,1)S(1)} %get-tuple-element.10.yrecv), custom_call_target="tpu_custom_call" | custom-call | tf_op jit(solution)/shard_map/pallas_call | solution.py:375

commit v7 on v6

--- a/solution.py
+++ b/solution.py
@@ -131,34 +131,43 @@
         return ids_ref[0:1, cols], ids_ref[1:2, cols], keep_ref[0:1, cols] == 1
 
     def route(on_block):
-        count = jnp.zeros((experts, TILE), jnp.float32)
+        bf16, f32 = jnp.bfloat16, jnp.float32
+        expert = lax.broadcasted_iota(jnp.int32, (experts, TILE), 0)
+        ones = jnp.ones((TILE, 128), bf16)
+        order = lax.broadcasted_iota(jnp.int32, (TILE, TILE), 0) < lax.broadcasted_iota(jnp.int32, (TILE, TILE), 1)
+        earlier = jnp.concatenate([jnp.where(order, 1.0, 0.0).astype(bf16), ones], axis=1)
+        packed_expert = expert.astype(f32).astype(bf16)
+
+        def one_hot(row):
+            return jnp.where(packed_expert == row.astype(f32).astype(bf16), bf16(1), bf16(0))
+
+        count = jnp.zeros((experts, TILE), bf16)
         for b in range(blocks):
-            i1, _, _ = load_ids(b)
-            count = count + hot(b, i1).astype(jnp.float32)
-        base1 = jnp.zeros((experts, 1), jnp.float32)
-        base2 = jnp.sum(count, axis=1, keepdims=True)
-        before = (
-            lax.broadcasted_iota(jnp.int32, (TILE, TILE), 0) < lax.broadcasted_iota(jnp.int32, (TILE, TILE), 1)
-        ).astype(jnp.bfloat16)
+            count = count + one_hot(load_ids(b)[0])
+        base1 = jnp.zeros((experts, 128), f32)
+        base2 = jnp.dot(count, ones, preferred_element_type=f32)
         for b in range(blocks):
             on_block(b)
             i1, i2, k2 = load_ids(b)
-            hot1 = hot(b, i1).astype(jnp.float32)
-            hot2 = jnp.where(k2, hot(b, i2).astype(jnp.float32), 0.0)
-            ahead1 = jnp.dot(hot1.astype(jnp.bfloat16), before, preferred_element_type=jnp.float32) + base1
-            ahead2 = jnp.dot(hot2.astype(jnp.bfloat16), before, preferred_element_type=jnp.float32) + base2
-            base1 = base1 + jnp.sum(hot1, axis=1, keepdims=True)
-            base2 = base2 + jnp.sum(hot2, axis=1, keepdims=True)
-            pos1 = jnp.sum(ahead1 * hot1, axis=0, keepdims=True)
-            pos2 = jnp.sum(ahead2 * hot2, axis=0, keepdims=True)
-
-            def code(e, pos, kept):
-                home = (e & (local - 1)) * rows + (e >> shift) * capacity
-                return jnp.where(kept, home.astype(jnp.float32) + pos, -1.0)
-
-            cols = pl.ds(b * TILE, TILE)
-            crow[0:1, cols] = code(i1, pos1, pos1 < capacity)
-            crow[1:2, cols] = code(i2, pos2, jnp.logical_and(k2, pos2 < capacity))
+            kept2 = jnp.where(k2, i2, -1)
+            hots = jnp.concatenate([one_hot(i1), one_hot(kept2)], axis=0)
+            ahead = jnp.dot(hots, earlier, preferred_element_type=f32)
+            ahead1, ahead2 = ahead[:experts], ahead[experts:]
+            for lane in range(0, TILE, 128):
+                part = slice(lane, lane + 128)
+                cols = pl.ds(b * TILE + lane, 128)
+                is1, is2 = expert[:, part] == i1[:, part], expert[:, part] == kept2[:, part]
+                pos1 = jnp.sum(jnp.where(is1, ahead1[:, part] + base1, 0.0), axis=0, keepdims=True)
+                pos2 = jnp.sum(jnp.where(is2, ahead2[:, part] + base2, 0.0), axis=0, keepdims=True)
+
+                def code(e, pos, kept):
+                    home = (e & (local - 1)) * rows + (e >> shift) * capacity
+                    return jnp.where(kept, home.astype(f32) + pos, -1.0)
+
+                crow[0:1, cols] = code(i1[:, part], pos1, pos1 < capacity)
+                crow[1:2, cols] = code(i2[:, part], pos2, jnp.logical_and(k2[:, part], pos2 < capacity))
+            base1 = base1 + ahead1[:, TILE:]
+            base2 = base2 + ahead2[:, TILE:]
 
     def gates():
         for b in range(blocks):
@@ -176,11 +185,16 @@
 
     def dispatch_mask(k):
         base = (k * rows).astype(jnp.float32)
+        want = lax.broadcasted_iota(jnp.int32, (rows, TILE), 0).astype(jnp.float32).astype(jnp.bfloat16)
         for b in range(blocks):
             cols = pl.ds(b * TILE, TILE)
-            want = lax.broadcasted_iota(jnp.int32, (rows, TILE), 0).astype(jnp.float32)
-            c1, c2 = crow[0:1, cols] - base, crow[1:2, cols] - base
-            dmat[:, cols] = jnp.where(jnp.logical_or(c1 == want, c2 == want), 1.0, 0.0).astype(jnp.bfloat16)
+
+            def row_of(q):
+                row = crow[q : q + 1, cols] - base
+                return jnp.where(jnp.logical_and(row >= 0.0, row < rows), row, -1.0).astype(jnp.bfloat16)
+
+            hit = jnp.logical_or(want == row_of(0), want == row_of(1))
+            dmat[:, cols] = jnp.where(hit, jnp.bfloat16(1), jnp.bfloat16(0))
 
     def dispatch_tile(slot, j):
         cols = pl.ds(pl.multiple_of(j * TILE, TILE), TILE)

time: 372 us -> 371 us (level)
  no operation moved by 1% of the time
where the time goes in v7:
time: 371 us
  Pallas kernels  371 us (100%)
    pallas_call x1, Pallas kernels, local_layer(): pl.pallas_call(functools.partial(moe_kernel, n, sizes), out_shape=(pltpu....  367 us

profile of v7, /device:TPU:113, one launch (start us, length us, event | category | flops | bytes accessed | tf_op | source)
XLA Modules:
  0.0 371.3 jit_solution(3473699834013273332)
XLA Ops:
  0.0 366.8 %shard_map.64 = (f32[2048,2048]{1,0:T(8,128)S(1)}, bf16[2048,256]{1,0:T(8,128)(2,1)S(1)}, bf16[4,256,2048]{2,1,0:T(8,128)(2,1)S(1)}) custom-call(s32[2,2048]{1,0:T(2,128)} %bitcast.3, s32[1,2048]{1,0:T(1,128)} %keep_hbm.1, bf16[1,2048,2048]{2,1,0:T(8,128)(2,1)} %x_hbm.1, bf16[2048,128]{1,0:T(8,128)(2,1)} %wg_hbm.1, bf16[16,2048,768]{2,1,0:T(8,128)(2,1)} %win_hbm.1, ...), custom_call_target="tpu_custom_call" | custom-call | tf_op jit(solution)/shard_map/pallas_call | solution.py:352
  366.8 4.5 %shard_map.65 = bf16[1,2048,2048]{2,1,0:T(8,128)(2,1)} custom-call(f32[2048,2048]{1,0:T(8,128)S(1)} %get-tuple-element.8.acc, bf16[2048,256]{1,0:T(8,128)(2,1)S(1)} %get-tuple-element.9.mix_last, bf16[4,256,2048]{2,1,0:T(8,128)(2,1)S(1)} %get-tuple-element.10.yrecv), custom_call_target="tpu_custom_call" | custom-call | tf_op jit(solution)/shard_map/pallas_call | solution.py:389

commit v8 on v7

--- a/solution.py
+++ b/solution.py
@@ -33,18 +33,16 @@
 def last_kernel(slot, acc, mix_last, yrecv, out_hbm, stage, sem):
     tokens, model = acc.shape
 
-    def out_copy(i):
-        toks = pl.ds(pl.multiple_of(i * TILE, TILE), TILE)
-        return pltpu.make_async_copy(stage.at[toks], out_hbm.at[0, toks], sem)
+    width = 2 * TILE
 
     @pl.loop(0, tokens // TILE)
     def _(i):
         toks = pl.ds(pl.multiple_of(i * TILE, TILE), TILE)
-        for j in range(0, model, 2 * TILE):
-            cols = pl.ds(j, 2 * TILE)
+        for j in range(0, model, width):
+            cols = pl.ds(j, width)
             got = acc[toks, cols] + jnp.dot(mix_last[toks, :], yrecv[slot, :, cols], preferred_element_type=jnp.float32)
             stage[toks, cols] = got.astype(jnp.bfloat16)
-        out_copy(i).start()
+            pltpu.make_async_copy(stage.at[toks, cols], out_hbm.at[0, toks, cols], sem).start()
 
     pltpu.make_async_copy(stage, out_hbm.at[0], sem).wait()
 

time: 371 us -> 371 us (level)
  no operation moved by 1% of the time
where the time goes in v8:
time: 371 us
  Pallas kernels  371 us (100%)
    pallas_call x1, Pallas kernels, local_layer(): pl.pallas_call(functools.partial(moe_kernel, n, sizes), out_shape=(pltpu....  367 us

profile of v8, /device:TPU:113, one launch (start us, length us, event | category | flops | bytes accessed | tf_op | source)
XLA Modules:
  0.0 371.1 jit_solution(305040104260583129)
XLA Ops:
  0.0 366.8 %shard_map.64 = (f32[2048,2048]{1,0:T(8,128)S(1)}, bf16[2048,256]{1,0:T(8,128)(2,1)S(1)}, bf16[4,256,2048]{2,1,0:T(8,128)(2,1)S(1)}) custom-call(s32[2,2048]{1,0:T(2,128)} %bitcast.3, s32[1,2048]{1,0:T(1,128)} %keep_hbm.1, bf16[1,2048,2048]{2,1,0:T(8,128)(2,1)} %x_hbm.1, bf16[2048,128]{1,0:T(8,128)(2,1)} %wg_hbm.1, bf16[16,2048,768]{2,1,0:T(8,128)(2,1)} %win_hbm.1, ...), custom_call_target="tpu_custom_call" | custom-call | tf_op jit(solution)/shard_map/pallas_call | solution.py:350
  366.8 4.3 %shard_map.65 = bf16[1,2048,2048]{2,1,0:T(8,128)(2,1)} custom-call(f32[2048,2048]{1,0:T(8,128)S(1)} %get-tuple-element.8.acc, bf16[2048,256]{1,0:T(8,128)(2,1)S(1)} %get-tuple-element.9.mix_last, bf16[4,256,2048]{2,1,0:T(8,128)(2,1)S(1)} %get-tuple-element.10.yrecv), custom_call_target="tpu_custom_call" | custom-call | tf_op jit(solution)/shard_map/pallas_call | solution.py:387

commit v9 on v8

--- a/solution.py
+++ b/solution.py
@@ -40,7 +40,9 @@
         toks = pl.ds(pl.multiple_of(i * TILE, TILE), TILE)
         for j in range(0, model, width):
             cols = pl.ds(j, width)
-            got = acc[toks, cols] + jnp.dot(mix_last[toks, :], yrecv[slot, :, cols], preferred_element_type=jnp.float32)
+            got = acc[toks, cols]
+            if j >= model // 2:
+                got += jnp.dot(mix_last[toks, :], yrecv[slot, :, cols], preferred_element_type=jnp.float32)
             stage[toks, cols] = got.astype(jnp.bfloat16)
             pltpu.make_async_copy(stage.at[toks, cols], out_hbm.at[0, toks, cols], sem).start()
 
@@ -90,24 +92,24 @@
                 continue
             targets.append(lax.rem(my_chip + dist, chips) * cores + lax.rem(my_core + c, cores))
 
-    def send(src, src_slot, dst, dst_slot, s_sem, r_sem, cols=slice(None)):
+    def send(src, src_slot, dst, dst_slot, s_sem, r_sem, cols=slice(None), own_sem=None):
         for d in targets:
             pltpu.make_async_remote_copy(
                 src_ref=src.at[src_slot, owner_rows(d), cols],
                 dst_ref=dst.at[dst_slot, owner_rows(me), cols],
-                send_sem=s_sem.at[src_slot],
-                recv_sem=r_sem.at[dst_slot],
+                send_sem=s_sem.at[src_slot if own_sem is None else own_sem[0]],
+                recv_sem=r_sem.at[dst_slot if own_sem is None else own_sem[1]],
                 device_id={"ep": d},
                 device_id_type=MESH,
             ).start()
 
-    def all_peers(src, src_slot, dst, dst_slot, s_sem, r_sem):
+    def all_peers(src, src_slot, dst, dst_slot, s_sem, r_sem, cols=slice(None), own_sem=None):
         part = pl.ds(0, (n - 1) * capacity)
         return pltpu.make_async_remote_copy(
-            src_ref=src.at[src_slot, part],
-            dst_ref=dst.at[dst_slot, part],
-            send_sem=s_sem.at[src_slot],
-            recv_sem=r_sem.at[dst_slot],
+            src_ref=src.at[src_slot, part, cols],
+            dst_ref=dst.at[dst_slot, part, cols],
+            send_sem=s_sem.at[src_slot if own_sem is None else own_sem[0]],
+            recv_sem=r_sem.at[dst_slot if own_sem is None else own_sem[1]],
             device_id={"ep": me},
             device_id_type=MESH,
         )
@@ -117,6 +119,12 @@
 
     def back_args(k):
         return (ysend, lax.rem(k, 2), yrecv, lax.rem(k, yslots), ys_sem, yr_sem)
+
+    half = model // 2
+    last_halves = (
+        (*back_args(jnp.int32(local - 1)), pl.ds(0, half)),
+        (*back_args(jnp.int32(local - 1)), pl.ds(half, half), (ys_sem.shape[0] - 1, yslots)),
+    )
 
     def keep_own(src, src_slot, dst, dst_slot, *_):
         dst[dst_slot, owner_rows(me), :] = src[src_slot, owner_rows(me), :]
@@ -214,11 +222,21 @@
             h = jnp.dot(frecv[slot], win_v[w, :, cols], preferred_element_type=jnp.float32)
             hid[:, cols] = jnp.maximum(h, 0.0).astype(jnp.bfloat16)
 
-        @pl.loop(0, model // TILE)
-        def _(j):
-            cols = pl.ds(pl.multiple_of(j * TILE, TILE), TILE)
-            y = jnp.dot(hid[...], wout_v[w, :, cols], preferred_element_type=jnp.float32)
-            ysend[out_slot, :, cols] = y.astype(jnp.bfloat16)
+        for h in range(2):
+
+            @pl.loop(h * half // TILE, (h + 1) * half // TILE)
+            def _(j):
+                cols = pl.ds(pl.multiple_of(j * TILE, TILE), TILE)
+                y = jnp.dot(hid[...], wout_v[w, :, cols], preferred_element_type=jnp.float32)
+                ysend[out_slot, :, cols] = y.astype(jnp.bfloat16)
+
+            @pl.when(k == local - 1)
+            def _():
+                send(*last_halves[h])
+
+        @pl.when(k < local - 1)
+        def _():
+            send(*back_args(k))
 
     def combine(k):
         @pl.loop(0, blocks)
@@ -269,7 +287,7 @@
     for copy in weight_copies(first):
         copy.start()
 
-    @pl.loop(0, local + LAG)
+    @pl.loop(0, local + LAG - 1)
     def _(t):
         @pl.when(t >= LAG)
         def _():
@@ -289,7 +307,7 @@
             def _(i):
                 acc[pl.ds(pl.multiple_of(i * TILE, TILE), TILE), :] = jnp.zeros((TILE, model), jnp.float32)
 
-        @pl.when(jnp.logical_and(t >= LAG, t < local + LAG - 1))
+        @pl.when(t >= LAG)
         def _():
             combine(t - LAG)
 
@@ -318,7 +336,6 @@
                 all_peers(*back_args(k - 2)).wait_send()
 
             experts_ffn(k)
-            send(*back_args(k))
             keep_own(*back_args(k))
 
         @pl.when(t + 1 < local)
@@ -329,9 +346,23 @@
 
             dispatch(t + 1)
 
+    all_peers(*last_halves[0]).wait_recv()
+
+    @pl.loop(0, blocks)
+    def _(i):
+        toks = pl.ds(pl.multiple_of(i * TILE, TILE), TILE)
+        for j in range(0, half, 2 * TILE):
+            cols = pl.ds(j, 2 * TILE)
+            acc[toks, cols] += jnp.dot(
+                mix_last[toks, :], yrecv[(local - 1) % yslots, :, cols], preferred_element_type=jnp.float32
+            )
+
+    all_peers(*last_halves[1]).wait_recv()
     for k in range(max(local - 2, 0), local):
         all_peers(*fwd_args(jnp.int32(k))).wait_send()
-        all_peers(*back_args(jnp.int32(k))).wait_send()
+    all_peers(*back_args(jnp.int32(local - 2))).wait_send()
+    for part in last_halves:
+        all_peers(*part).wait_send()
 
 
 def solution(mesh):
@@ -377,8 +408,8 @@
                 dma((2,)),
                 dma((2,)),
                 dma((LAG,)),
-                dma((2,)),
-                dma((LAG + 1,)),
+                dma((3,)),
+                dma((LAG + 2,)),
             ],
             compiler_params=pltpu.CompilerParams(
                 collective_id=0, has_side_effects=True, vmem_limit_bytes=VMEM_A

time: 371 us -> 370 us (level)
  no operation moved by 1% of the time
where the time goes in v9:
time: 370 us
  Pallas kernels  370 us (100%)
    pallas_call x1, Pallas kernels, local_layer(): pl.pallas_call(functools.partial(moe_kernel, n, sizes), out_shape=(pltpu....  367 us

profile of v9, /device:TPU:113, one launch (start us, length us, event | category | flops | bytes accessed | tf_op | source)
XLA Modules:
  0.0 370.2 jit_solution(7733502458447650829)
XLA Ops:
  0.0 366.8 %shard_map.64 = (f32[2048,2048]{1,0:T(8,128)S(1)}, bf16[2048,256]{1,0:T(8,128)(2,1)S(1)}, bf16[4,256,2048]{2,1,0:T(8,128)(2,1)S(1)}) custom-call(s32[2,2048]{1,0:T(2,128)} %bitcast.3, s32[1,2048]{1,0:T(1,128)} %keep_hbm.1, bf16[1,2048,2048]{2,1,0:T(8,128)(2,1)} %x_hbm.1, bf16[2048,128]{1,0:T(8,128)(2,1)} %wg_hbm.1, bf16[16,2048,768]{2,1,0:T(8,128)(2,1)} %win_hbm.1, ...), custom_call_target="tpu_custom_call" | custom-call | tf_op jit(solution)/shard_map/pallas_call | solution.py:381
  366.8 3.4 shard_map.65
